TPU v7x, 8 devices: a whole 2x2x1 slice. The times are simulated.
8 devices in a mesh: replica: 4 (over z, y, x), data: 2 (over core).
Axes of the slice: x: 2, y: 2, z: 1, core: 2. Of those that a mesh axis runs over, the one named last changes fastest.
Arguments:
- img_x: bfloat16 [32768, 1280], P(('replica', 'data'))
- txt_x: bfloat16 [32768, 1024], P(('replica', 'data'))
- w_img: bfloat16 [1280, 1024], replicated
- w_txt: bfloat16 [1024, 1024], replicated
- log_temp: float32 [1], replicated
- logit_bias: float32 [1], replicated
Outputs:
- output 1: float32 [1], replicated
- output 2: float32 [1], replicated
- output 3: float32 [1], replicated
- output 4: float32 [1280, 1024], replicated
- output 5: float32 [1024, 1024], replicated
All inputs are finite; a program needn't handle non-finite values.
Results may differ from a plain program's by a relative error of at most 0.001.
Values are sent between devices in bfloat16 or wider.
A program may use at most 1 GiB of HBM per device.

v0:
```python
import jax
import jax.numpy as jnp
from jax import lax
from jax.sharding import PartitionSpec as P


def normalize(raw):
    return raw * lax.rsqrt(jnp.sum(raw * raw, axis=-1, keepdims=True))


def embed_rows(feat_x, w_proj):
    raw_emb = jnp.dot(feat_x, w_proj, preferred_element_type=jnp.float32)
    unit_emb, pull_back = jax.vjp(normalize, raw_emb)
    return unit_emb.astype(jnp.bfloat16), pull_back


def tile_terms(img_emb, txt_blk, labels, temp_scale, bias_val, total_rows):
    sim_tile = jnp.einsum("id,jd->ij", img_emb, txt_blk, preferred_element_type=jnp.float32)
    logits = temp_scale * sim_tile + bias_val
    loss_part = -jnp.sum(jax.nn.log_sigmoid(labels * logits))
    grad_tile = -labels * jax.nn.sigmoid(-labels * logits) / total_rows
    grad_b = grad_tile.astype(jnp.bfloat16)
    d_img = jnp.dot(grad_b, txt_blk, preferred_element_type=jnp.float32)
    d_txt = jnp.einsum("ij,id->jd", grad_b, img_emb, preferred_element_type=jnp.float32)
    return loss_part, jnp.sum(grad_tile * sim_tile), jnp.sum(grad_tile), d_img, d_txt


def solution(mesh):
    rep_count = mesh.shape["replica"]
    data_count = mesh.shape["data"]
    dev_count = rep_count * data_count
    batch_axes = ("replica", "data")
    next_perm = [(k, (k + 1) % dev_count) for k in range(dev_count)]

    def local_fn(img_x, txt_x, w_img, w_txt, log_temp, logit_bias):
        local_rows = img_x.shape[0]
        total_rows = local_rows * dev_count
        img_emb, img_pull = embed_rows(img_x, w_img)
        txt_emb, txt_pull = embed_rows(txt_x, w_txt)
        temp_scale = jnp.exp(log_temp[0])
        bias_val = logit_bias[0]
        row_ids = lax.broadcasted_iota(jnp.int32, (local_rows, 1), 0)
        col_ids = lax.broadcasted_iota(jnp.int32, (1, local_rows), 1)
        diag_labels = jnp.where(row_ids == col_ids, 1.0, -1.0)
        first = tile_terms(img_emb, txt_emb, diag_labels, temp_scale, bias_val, total_rows)

        def hop(step, state):
            txt_blk, d_txt_acc, d_img_acc, loss_acc, temp_acc, bias_acc = state
            txt_blk = lax.ppermute(txt_blk, batch_axes, next_perm)
            d_txt_acc = lax.ppermute(d_txt_acc, batch_axes, next_perm)
            loss_part, temp_part, bias_part, d_img_part, d_txt_part = tile_terms(img_emb, txt_blk, -1.0, temp_scale, bias_val, total_rows)
            return (txt_blk, d_txt_acc + d_txt_part, d_img_acc + d_img_part, loss_acc + loss_part, temp_acc + temp_part, bias_acc + bias_part)

        init_state = (txt_emb, first[4], first[3], first[0], first[1], first[2])
        final_state = lax.fori_loop(1, dev_count, hop, init_state)
        d_txt_home = lax.ppermute(final_state[1], batch_axes, next_perm)
        d_img_raw = img_pull(temp_scale * final_state[2])[0].astype(jnp.bfloat16)
        d_txt_raw = txt_pull(temp_scale * d_txt_home)[0].astype(jnp.bfloat16)
        d_w_img = jnp.einsum("nf,nd->fd", img_x, d_img_raw, preferred_element_type=jnp.float32)
        d_w_txt = jnp.einsum("nf,nd->fd", txt_x, d_txt_raw, preferred_element_type=jnp.float32)
        loss_total, temp_total, bias_total, d_w_img, d_w_txt = lax.psum((final_state[3], final_state[4], final_state[5], d_w_img, d_w_txt), batch_axes)
        loss_out = jnp.reshape(loss_total / total_rows, (1,))
        d_log_temp = jnp.reshape(temp_scale * temp_total, (1,))
        d_logit_bias = jnp.reshape(bias_total, (1,))
        return loss_out, d_log_temp, d_logit_bias, d_w_img, d_w_txt

    batch_spec = P(batch_axes, None)
    return jax.shard_map(local_fn, mesh=mesh, in_specs=(batch_spec, batch_spec, P(), P(), P(), P()), out_specs=(P(), P(), P(), P(), P()), check_vma=False)
```

profile of v0, /device:TPU:0, one launch (start us, length us, event | category | flops | bytes accessed | tf_op | source)
XLA Modules:
  0.0 3003.3 jit_solution(7227814101144093876)
XLA Ops:
  8.9 17.2 multiply_reduce_fusion.4
  56.0 132.8 %fusion.43 = (f32[]{:T(128)}, f32[]{:T(128)}, f32[]{:T(128)}, bf16[4096,4096]{1,0:T(8,128)(2,1)}) fusion(f32[]{:T(128)} %bitcast.33, f32[]{:T(128)} %bitcast, bf16[4096,1024]{0,1:T(8,128)(2,1)S(1)} %multiply_convert_fusion, bf16[4096,1024]{0,1:T(8,128)(2,1)S(1)} %multiply_convert_fusion.1), kind=kOutput, calls=%fused_computation.53 | convolution fusion | flops 34762391552 | bytes 50331668 | tf_op jit(solution)/shard_map/id,jd->ij/dot_general | solution.py:18
  188.7 43.1 %fusion.23 = f32[4096,1024]{1,0:T(8,128)} fusion(bf16[4096,1024]{0,1:T(8,128)(2,1)} %copy-done.4, bf16[4096,4096]{1,0:T(8,128)(2,1)} %get-tuple-element.112), kind=kOutput, calls=%fused_computation.33 | convolution fusion | flops 34359738368 | bytes 58720256 | tf_op jit(solution)/shard_map/dot_general | solution.py:23
  231.9 43.6 %fusion.25 = f32[4096,1024]{1,0:T(8,128)} fusion(bf16[4096,1024]{0,1:T(8,128)(2,1)} %copy-done.3, bf16[4096,4096]{1,0:T(8,128)(2,1)} %get-tuple-element.112), kind=kOutput, calls=%fused_computation.35 | convolution fusion | flops 34359738368 | bytes 58720256 | tf_op jit(solution)/shard_map/ij,id->jd/dot_general | solution.py:24
  299.3 2290.2 %while.20 = (s32[]{:T(128)}, bf16[4096,1024]{1,0:T(8,128)(2,1)}, f32[4096,1024]{1,0:T(8,128)}, f32[4096,1024]{1,0:T(8,128)}, f32[]{:T(128)}, /*index=5*/f32[]{:T...) while((s32[]{:T(128)}, bf16[4096,1024]{1,0:T(8,128)(2,1)}, ...), condition=%wide.region_9.10_spmd, body=%wide.region_5.9_spmd.sunk | while | flops 103624474624 | bytes 419430624 | solution.py:55
  303.0 91.4 %collective-permute-done = bf16[4096,1024]{1,0:T(8,128)(2,1)} collective-permute-done((bf16[4096,1024]{1,0:T(8,128)(2,1)}, bf16[4096,1024]{1,0:T(8,128)(2,1)}, u32[]{:S(2)}, u32[]{:S(2)}) %collective-permute-start) | collective-permute-done | bytes 8388640 | tf_op jit(solution)/shard_map/while/body/eval_jaxpr/ppermute | solution.py:49
  394.4 97.5 %fusion.76 = (f32[]{:T(128)}, f32[]{:T(128)}, f32[]{:T(128)}, f32[4096,4096]{1,0:T(8,128)}) fusion(f32[]{:T(128)} %get-tuple-element.224, f32[]{:T(128)} %get-tuple-element.222, bf16[4096,1024]{1,0:T(8,128)(2,1)} %get-tuple-element.223, bf16[4096,1024]{1,0:T(8,128)(2,1)} %collective-permute-done), kind=kOutput, calls=%fused_computation.11.clone.1 | convolution fusion | flops 34661728256 | bytes 83886096 | tf_op jit(solution)/shard_map/while/body/eval_jaxpr/id,jd->ij/dot_general | solution.py:18
  503.2 46.7 %fusion.78 = f32[4096,1024]{1,0:T(8,128)} fusion(f32[4096,1024]{1,0:T(8,128)} %get-tuple-element.207, bf16[4096,1024]{1,0:T(8,128)(2,1)} %collective-permute-done, f32[4096,4096]{1,0:T(8,128)} %get-tuple-element.189, f32[]{:T(128)} %get-tuple-element.224, f32[]{:T(128)} %get-tuple-element.222), kind=kOutput, calls=%fused_computation.10.clone.1 | convolution fusion | flops 34481373184 | bytes 109051912 | tf_op jit(solution)/shard_map/while/body/eval_jaxpr/dot_general | solution.py:23
  549.9 24.2 collective-permute-done.1
  574.2 50.7 %fusion.77 = f32[4096,1024]{1,0:T(8,128)} fusion(f32[4096,1024]{1,0:T(8,128)} %collective-permute-done.1, bf16[4096,1024]{1,0:T(8,128)(2,1)} %get-tuple-element.223, f32[4096,4096]{1,0:T(8,128)} %get-tuple-element.189, f32[]{:T(128)} %get-tuple-element.224, f32[]{:T(128)} %get-tuple-element.222), kind=kOutput, calls=%fused_computation.9.clone.1 | convolution fusion | flops 34481373184 | bytes 109051912 | tf_op jit(solution)/shard_map/while/body/eval_jaxpr/ij,id->jd/dot_general | solution.py:24
  627.8 92.3 %collective-permute-done = bf16[4096,1024]{1,0:T(8,128)(2,1)} collective-permute-done((bf16[4096,1024]{1,0:T(8,128)(2,1)}, bf16[4096,1024]{1,0:T(8,128)(2,1)}, u32[]{:S(2)}, u32[]{:S(2)}) %collective-permute-start) | collective-permute-done | bytes 8388640 | tf_op jit(solution)/shard_map/while/body/eval_jaxpr/ppermute | solution.py:49
  720.1 97.5 %fusion.76 = (f32[]{:T(128)}, f32[]{:T(128)}, f32[]{:T(128)}, f32[4096,4096]{1,0:T(8,128)}) fusion(f32[]{:T(128)} %get-tuple-element.224, f32[]{:T(128)} %get-tuple-element.222, bf16[4096,1024]{1,0:T(8,128)(2,1)} %get-tuple-element.223, bf16[4096,1024]{1,0:T(8,128)(2,1)} %collective-permute-done), kind=kOutput, calls=%fused_computation.11.clone.1 | convolution fusion | flops 34661728256 | bytes 83886096 | tf_op jit(solution)/shard_map/while/body/eval_jaxpr/id,jd->ij/dot_general | solution.py:18
  828.9 46.7 %fusion.78 = f32[4096,1024]{1,0:T(8,128)} fusion(f32[4096,1024]{1,0:T(8,128)} %get-tuple-element.207, bf16[4096,1024]{1,0:T(8,128)(2,1)} %collective-permute-done, f32[4096,4096]{1,0:T(8,128)} %get-tuple-element.189, f32[]{:T(128)} %get-tuple-element.224, f32[]{:T(128)} %get-tuple-element.222), kind=kOutput, calls=%fused_computation.10.clone.1 | convolution fusion | flops 34481373184 | bytes 109051912 | tf_op jit(solution)/shard_map/while/body/eval_jaxpr/dot_general | solution.py:23
  875.6 24.3 collective-permute-done.1
  899.9 50.7 %fusion.77 = f32[4096,1024]{1,0:T(8,128)} fusion(f32[4096,1024]{1,0:T(8,128)} %collective-permute-done.1, bf16[4096,1024]{1,0:T(8,128)(2,1)} %get-tuple-element.223, f32[4096,4096]{1,0:T(8,128)} %get-tuple-element.189, f32[]{:T(128)} %get-tuple-element.224, f32[]{:T(128)} %get-tuple-element.222), kind=kOutput, calls=%fused_computation.9.clone.1 | convolution fusion | flops 34481373184 | bytes 109051912 | tf_op jit(solution)/shard_map/while/body/eval_jaxpr/ij,id->jd/dot_general | solution.py:24
  952.6 93.2 %collective-permute-done = bf16[4096,1024]{1,0:T(8,128)(2,1)} collective-permute-done((bf16[4096,1024]{1,0:T(8,128)(2,1)}, bf16[4096,1024]{1,0:T(8,128)(2,1)}, u32[]{:S(2)}, u32[]{:S(2)}) %collective-permute-start) | collective-permute-done | bytes 8388640 | tf_op jit(solution)/shard_map/while/body/eval_jaxpr/ppermute | solution.py:49
  1045.8 97.5 %fusion.76 = (f32[]{:T(128)}, f32[]{:T(128)}, f32[]{:T(128)}, f32[4096,4096]{1,0:T(8,128)}) fusion(f32[]{:T(128)} %get-tuple-element.224, f32[]{:T(128)} %get-tuple-element.222, bf16[4096,1024]{1,0:T(8,128)(2,1)} %get-tuple-element.223, bf16[4096,1024]{1,0:T(8,128)(2,1)} %collective-permute-done), kind=kOutput, calls=%fused_computation.11.clone.1 | convolution fusion | flops 34661728256 | bytes 83886096 | tf_op jit(solution)/shard_map/while/body/eval_jaxpr/id,jd->ij/dot_general | solution.py:18
  1154.6 46.7 %fusion.78 = f32[4096,1024]{1,0:T(8,128)} fusion(f32[4096,1024]{1,0:T(8,128)} %get-tuple-element.207, bf16[4096,1024]{1,0:T(8,128)(2,1)} %collective-permute-done, f32[4096,4096]{1,0:T(8,128)} %get-tuple-element.189, f32[]{:T(128)} %get-tuple-element.224, f32[]{:T(128)} %get-tuple-element.222), kind=kOutput, calls=%fused_computation.10.clone.1 | convolution fusion | flops 34481373184 | bytes 109051912 | tf_op jit(solution)/shard_map/while/body/eval_jaxpr/dot_general | solution.py:23
  1201.3 24.3 collective-permute-done.1
  1225.6 50.7 %fusion.77 = f32[4096,1024]{1,0:T(8,128)} fusion(f32[4096,1024]{1,0:T(8,128)} %collective-permute-done.1, bf16[4096,1024]{1,0:T(8,128)(2,1)} %get-tuple-element.223, f32[4096,4096]{1,0:T(8,128)} %get-tuple-element.189, f32[]{:T(128)} %get-tuple-element.224, f32[]{:T(128)} %get-tuple-element.222), kind=kOutput, calls=%fused_computation.9.clone.1 | convolution fusion | flops 34481373184 | bytes 109051912 | tf_op jit(solution)/shard_map/while/body/eval_jaxpr/ij,id->jd/dot_general | solution.py:24
  1277.8 93.8 %collective-permute-done = bf16[4096,1024]{1,0:T(8,128)(2,1)} collective-permute-done((bf16[4096,1024]{1,0:T(8,128)(2,1)}, bf16[4096,1024]{1,0:T(8,128)(2,1)}, u32[]{:S(2)}, u32[]{:S(2)}) %collective-permute-start) | collective-permute-done | bytes 8388640 | tf_op jit(solution)/shard_map/while/body/eval_jaxpr/ppermute | solution.py:49
  1371.5 97.5 %fusion.76 = (f32[]{:T(128)}, f32[]{:T(128)}, f32[]{:T(128)}, f32[4096,4096]{1,0:T(8,128)}) fusion(f32[]{:T(128)} %get-tuple-element.224, f32[]{:T(128)} %get-tuple-element.222, bf16[4096,1024]{1,0:T(8,128)(2,1)} %get-tuple-element.223, bf16[4096,1024]{1,0:T(8,128)(2,1)} %collective-permute-done), kind=kOutput, calls=%fused_computation.11.clone.1 | convolution fusion | flops 34661728256 | bytes 83886096 | tf_op jit(solution)/shard_map/while/body/eval_jaxpr/id,jd->ij/dot_general | solution.py:18
  1480.4 46.7 %fusion.78 = f32[4096,1024]{1,0:T(8,128)} fusion(f32[4096,1024]{1,0:T(8,128)} %get-tuple-element.207, bf16[4096,1024]{1,0:T(8,128)(2,1)} %collective-permute-done, f32[4096,4096]{1,0:T(8,128)} %get-tuple-element.189, f32[]{:T(128)} %get-tuple-element.224, f32[]{:T(128)} %get-tuple-element.222), kind=kOutput, calls=%fused_computation.10.clone.1 | convolution fusion | flops 34481373184 | bytes 109051912 | tf_op jit(solution)/shard_map/while/body/eval_jaxpr/dot_general | solution.py:23
  1527.1 24.3 collective-permute-done.1
  1551.3 50.7 %fusion.77 = f32[4096,1024]{1,0:T(8,128)} fusion(f32[4096,1024]{1,0:T(8,128)} %collective-permute-done.1, bf16[4096,1024]{1,0:T(8,128)(2,1)} %get-tuple-element.223, f32[4096,4096]{1,0:T(8,128)} %get-tuple-element.189, f32[]{:T(128)} %get-tuple-element.224, f32[]{:T(128)} %get-tuple-element.222), kind=kOutput, calls=%fused_computation.9.clone.1 | convolution fusion | flops 34481373184 | bytes 109051912 | tf_op jit(solution)/shard_map/while/body/eval_jaxpr/ij,id->jd/dot_general | solution.py:24
  1603.5 93.8 %collective-permute-done = bf16[4096,1024]{1,0:T(8,128)(2,1)} collective-permute-done((bf16[4096,1024]{1,0:T(8,128)(2,1)}, bf16[4096,1024]{1,0:T(8,128)(2,1)}, u32[]{:S(2)}, u32[]{:S(2)}) %collective-permute-start) | collective-permute-done | bytes 8388640 | tf_op jit(solution)/shard_map/while/body/eval_jaxpr/ppermute | solution.py:49
  1697.3 97.5 %fusion.76 = (f32[]{:T(128)}, f32[]{:T(128)}, f32[]{:T(128)}, f32[4096,4096]{1,0:T(8,128)}) fusion(f32[]{:T(128)} %get-tuple-element.224, f32[]{:T(128)} %get-tuple-element.222, bf16[4096,1024]{1,0:T(8,128)(2,1)} %get-tuple-element.223, bf16[4096,1024]{1,0:T(8,128)(2,1)} %collective-permute-done), kind=kOutput, calls=%fused_computation.11.clone.1 | convolution fusion | flops 34661728256 | bytes 83886096 | tf_op jit(solution)/shard_map/while/body/eval_jaxpr/id,jd->ij/dot_general | solution.py:18
  1806.1 46.7 %fusion.78 = f32[4096,1024]{1,0:T(8,128)} fusion(f32[4096,1024]{1,0:T(8,128)} %get-tuple-element.207, bf16[4096,1024]{1,0:T(8,128)(2,1)} %collective-permute-done, f32[4096,4096]{1,0:T(8,128)} %get-tuple-element.189, f32[]{:T(128)} %get-tuple-element.224, f32[]{:T(128)} %get-tuple-element.222), kind=kOutput, calls=%fused_computation.10.clone.1 | convolution fusion | flops 34481373184 | bytes 109051912 | tf_op jit(solution)/shard_map/while/body/eval_jaxpr/dot_general | solution.py:23
  1852.8 24.3 collective-permute-done.1
  1877.0 50.7 %fusion.77 = f32[4096,1024]{1,0:T(8,128)} fusion(f32[4096,1024]{1,0:T(8,128)} %collective-permute-done.1, bf16[4096,1024]{1,0:T(8,128)(2,1)} %get-tuple-element.223, f32[4096,4096]{1,0:T(8,128)} %get-tuple-element.189, f32[]{:T(128)} %get-tuple-element.224, f32[]{:T(128)} %get-tuple-element.222), kind=kOutput, calls=%fused_computation.9.clone.1 | convolution fusion | flops 34481373184 | bytes 109051912 | tf_op jit(solution)/shard_map/while/body/eval_jaxpr/ij,id->jd/dot_general | solution.py:24
  1929.2 93.8 %collective-permute-done = bf16[4096,1024]{1,0:T(8,128)(2,1)} collective-permute-done((bf16[4096,1024]{1,0:T(8,128)(2,1)}, bf16[4096,1024]{1,0:T(8,128)(2,1)}, u32[]{:S(2)}, u32[]{:S(2)}) %collective-permute-start) | collective-permute-done | bytes 8388640 | tf_op jit(solution)/shard_map/while/body/eval_jaxpr/ppermute | solution.py:49
  2023.0 97.5 %fusion.76 = (f32[]{:T(128)}, f32[]{:T(128)}, f32[]{:T(128)}, f32[4096,4096]{1,0:T(8,128)}) fusion(f32[]{:T(128)} %get-tuple-element.224, f32[]{:T(128)} %get-tuple-element.222, bf16[4096,1024]{1,0:T(8,128)(2,1)} %get-tuple-element.223, bf16[4096,1024]{1,0:T(8,128)(2,1)} %collective-permute-done), kind=kOutput, calls=%fused_computation.11.clone.1 | convolution fusion | flops 34661728256 | bytes 83886096 | tf_op jit(solution)/shard_map/while/body/eval_jaxpr/id,jd->ij/dot_general | solution.py:18
  2131.8 46.7 %fusion.78 = f32[4096,1024]{1,0:T(8,128)} fusion(f32[4096,1024]{1,0:T(8,128)} %get-tuple-element.207, bf16[4096,1024]{1,0:T(8,128)(2,1)} %collective-permute-done, f32[4096,4096]{1,0:T(8,128)} %get-tuple-element.189, f32[]{:T(128)} %get-tuple-element.224, f32[]{:T(128)} %get-tuple-element.222), kind=kOutput, calls=%fused_computation.10.clone.1 | convolution fusion | flops 34481373184 | bytes 109051912 | tf_op jit(solution)/shard_map/while/body/eval_jaxpr/dot_general | solution.py:23
  2178.5 24.3 collective-permute-done.1
  2202.7 50.7 %fusion.77 = f32[4096,1024]{1,0:T(8,128)} fusion(f32[4096,1024]{1,0:T(8,128)} %collective-permute-done.1, bf16[4096,1024]{1,0:T(8,128)(2,1)} %get-tuple-element.223, f32[4096,4096]{1,0:T(8,128)} %get-tuple-element.189, f32[]{:T(128)} %get-tuple-element.224, f32[]{:T(128)} %get-tuple-element.222), kind=kOutput, calls=%fused_computation.9.clone.1 | convolution fusion | flops 34481373184 | bytes 109051912 | tf_op jit(solution)/shard_map/while/body/eval_jaxpr/ij,id->jd/dot_general | solution.py:24
  2254.9 93.8 %collective-permute-done = bf16[4096,1024]{1,0:T(8,128)(2,1)} collective-permute-done((bf16[4096,1024]{1,0:T(8,128)(2,1)}, bf16[4096,1024]{1,0:T(8,128)(2,1)}, u32[]{:S(2)}, u32[]{:S(2)}) %collective-permute-start) | collective-permute-done | bytes 8388640 | tf_op jit(solution)/shard_map/while/body/eval_jaxpr/ppermute | solution.py:49
  2348.7 97.5 %fusion.76 = (f32[]{:T(128)}, f32[]{:T(128)}, f32[]{:T(128)}, f32[4096,4096]{1,0:T(8,128)}) fusion(f32[]{:T(128)} %get-tuple-element.224, f32[]{:T(128)} %get-tuple-element.222, bf16[4096,1024]{1,0:T(8,128)(2,1)} %get-tuple-element.223, bf16[4096,1024]{1,0:T(8,128)(2,1)} %collective-permute-done), kind=kOutput, calls=%fused_computation.11.clone.1 | convolution fusion | flops 34661728256 | bytes 83886096 | tf_op jit(solution)/shard_map/while/body/eval_jaxpr/id,jd->ij/dot_general | solution.py:18
  2457.5 46.7 %fusion.78 = f32[4096,1024]{1,0:T(8,128)} fusion(f32[4096,1024]{1,0:T(8,128)} %get-tuple-element.207, bf16[4096,1024]{1,0:T(8,128)(2,1)} %collective-permute-done, f32[4096,4096]{1,0:T(8,128)} %get-tuple-element.189, f32[]{:T(128)} %get-tuple-element.224, f32[]{:T(128)} %get-tuple-element.222), kind=kOutput, calls=%fused_computation.10.clone.1 | convolution fusion | flops 34481373184 | bytes 109051912 | tf_op jit(solution)/shard_map/while/body/eval_jaxpr/dot_general | solution.py:23
  2504.2 24.3 collective-permute-done.1
  2528.4 50.7 %fusion.77 = f32[4096,1024]{1,0:T(8,128)} fusion(f32[4096,1024]{1,0:T(8,128)} %collective-permute-done.1, bf16[4096,1024]{1,0:T(8,128)(2,1)} %get-tuple-element.223, f32[4096,4096]{1,0:T(8,128)} %get-tuple-element.189, f32[]{:T(128)} %get-tuple-element.224, f32[]{:T(128)} %get-tuple-element.222), kind=kOutput, calls=%fused_computation.9.clone.1 | convolution fusion | flops 34481373184 | bytes 109051912 | tf_op jit(solution)/shard_map/while/body/eval_jaxpr/ij,id->jd/dot_general | solution.py:24
  2589.6 17.5 copy.14
  2607.0 17.5 copy.13
  2624.5 166.2 %collective-permute-done.2 = f32[4096,1024]{0,1:T(8,128)} collective-permute-done((f32[4096,1024]{0,1:T(8,128)}, f32[4096,1024]{0,1:T(8,128)}, u32[]{:S(2)}, u32[]{:S(2)}) %collective-permute-start.2) | collective-permute-done | bytes 16777248 | tf_op jit(solution)/shard_map/ppermute | solution.py:56
  2790.7 22.3 multiply_reduce_fusion.2
  2813.1 22.5 fusion.37
  2835.6 18.9 fusion.40
  2854.5 23.7 all-reduce
  2879.5 103.3 %all-reduce.4.cloned.1.call-done = (f32[1280,1024]{0,1:T(8,128)}, f32[1024,1024]{0,1:T(8,128)}) async-done(((f32[1280,1024]{0,1:T(8,128)}, f32[1024,1024]{0,1:T(8,128)}), (f32[1280,1024]{0,1:T(8,128)}, f32[1024,1024]{0,1:T(8,128)})) %all-reduce.4.cloned.1.call-update) | async-done | bytes 9437200 | tf_op jit(solution)/shard_map/psum | solution.py:61
  (63 shorter events, 123.5 us)
Async XLA Ops:
  7.2 1.8 copy-start
  7.2 2975.6 %all-reduce.4.cloned.1.call-start = ((), (), s32[]{:S(2)}) async-start(), calls=%async_computation | async-start | bytes 18874368 | tf_op jit(solution)/shard_map/psum | solution.py:61
  8.9 17.8 copy-start.13
  26.1 0.6 copy-start.5
  26.7 16.4 copy-start.11
  41.5 14.5 copy-start.7
  41.5 12.1 copy-start.2
  41.5 14.5 copy-start.9
  50.6 138.1 %copy-start.3 = (bf16[4096,1024]{0,1:T(8,128)(2,1)}, bf16[4096,1024]{0,1:T(8,128)(2,1)S(1)}, u32[]{:S(2)}) copy-start(bf16[4096,1024]{0,1:T(8,128)(2,1)S(1)} %multiply_convert_fusion) | copy-start | bytes 25165828
  56.0 132.8 %copy-start.4 = (bf16[4096,1024]{0,1:T(8,128)(2,1)}, bf16[4096,1024]{0,1:T(8,128)(2,1)S(1)}, u32[]{:S(2)}) copy-start(bf16[4096,1024]{0,1:T(8,128)(2,1)S(1)} %multiply_convert_fusion.1) | copy-start | bytes 25165828
  299.5 94.9 %collective-permute-start = (bf16[4096,1024]{1,0:T(8,128)(2,1)}, bf16[4096,1024]{1,0:T(8,128)(2,1)}, u32[]{:S(2)}, u32[]{:S(2)}) collective-permute-start(bf16[4096,1024]{1,0:T(8,128)(2,1)} %get-tuple-element.205), channel_id=1, source_target_pairs={{0,1},{1,2},{2,3},{3,4},{4,5},{5,6},{6,7},{7,0}} | collective-permute-start | bytes 25165832 | tf_op jit(solution)/shard_map/while/body/eval_jaxpr/ppermute | solution.py:49
  300.4 273.8 %collective-permute-start.1 = (f32[4096,1024]{1,0:T(8,128)}, f32[4096,1024]{1,0:T(8,128)}, u32[]{:S(2)}, u32[]{:S(2)}) collective-permute-start(f32[4096,1024]{1,0:T(8,128)} %get-tuple-element.206), channel_id=1, source_target_pairs={{0,1},{1,2},{2,3},{3,4},{4,5},{5,6},{6,7},{7,0}} | collective-permute-start | bytes 50331656 | tf_op jit(solution)/shard_map/while/body/eval_jaxpr/ppermute | solution.py:50
  626.4 93.8 %collective-permute-start = (bf16[4096,1024]{1,0:T(8,128)(2,1)}, bf16[4096,1024]{1,0:T(8,128)(2,1)}, u32[]{:S(2)}, u32[]{:S(2)}) collective-permute-start(bf16[4096,1024]{1,0:T(8,128)(2,1)} %get-tuple-element.205), channel_id=1, source_target_pairs={{0,1},{1,2},{2,3},{3,4},{4,5},{5,6},{6,7},{7,0}} | collective-permute-start | bytes 25165832 | tf_op jit(solution)/shard_map/while/body/eval_jaxpr/ppermute | solution.py:49
  626.4 273.5 %collective-permute-start.1 = (f32[4096,1024]{1,0:T(8,128)}, f32[4096,1024]{1,0:T(8,128)}, u32[]{:S(2)}, u32[]{:S(2)}) collective-permute-start(f32[4096,1024]{1,0:T(8,128)} %get-tuple-element.206), channel_id=1, source_target_pairs={{0,1},{1,2},{2,3},{3,4},{4,5},{5,6},{6,7},{7,0}} | collective-permute-start | bytes 50331656 | tf_op jit(solution)/shard_map/while/body/eval_jaxpr/ppermute | solution.py:50
  952.1 93.8 %collective-permute-start = (bf16[4096,1024]{1,0:T(8,128)(2,1)}, bf16[4096,1024]{1,0:T(8,128)(2,1)}, u32[]{:S(2)}, u32[]{:S(2)}) collective-permute-start(bf16[4096,1024]{1,0:T(8,128)(2,1)} %get-tuple-element.205), channel_id=1, source_target_pairs={{0,1},{1,2},{2,3},{3,4},{4,5},{5,6},{6,7},{7,0}} | collective-permute-start | bytes 25165832 | tf_op jit(solution)/shard_map/while/body/eval_jaxpr/ppermute | solution.py:49
  952.1 273.5 %collective-permute-start.1 = (f32[4096,1024]{1,0:T(8,128)}, f32[4096,1024]{1,0:T(8,128)}, u32[]{:S(2)}, u32[]{:S(2)}) collective-permute-start(f32[4096,1024]{1,0:T(8,128)} %get-tuple-element.206), channel_id=1, source_target_pairs={{0,1},{1,2},{2,3},{3,4},{4,5},{5,6},{6,7},{7,0}} | collective-permute-start | bytes 50331656 | tf_op jit(solution)/shard_map/while/body/eval_jaxpr/ppermute | solution.py:50
  1277.8 93.8 %collective-permute-start = (bf16[4096,1024]{1,0:T(8,128)(2,1)}, bf16[4096,1024]{1,0:T(8,128)(2,1)}, u32[]{:S(2)}, u32[]{:S(2)}) collective-permute-start(bf16[4096,1024]{1,0:T(8,128)(2,1)} %get-tuple-element.205), channel_id=1, source_target_pairs={{0,1},{1,2},{2,3},{3,4},{4,5},{5,6},{6,7},{7,0}} | collective-permute-start | bytes 25165832 | tf_op jit(solution)/shard_map/while/body/eval_jaxpr/ppermute | solution.py:49
  1277.8 273.5 %collective-permute-start.1 = (f32[4096,1024]{1,0:T(8,128)}, f32[4096,1024]{1,0:T(8,128)}, u32[]{:S(2)}, u32[]{:S(2)}) collective-permute-start(f32[4096,1024]{1,0:T(8,128)} %get-tuple-element.206), channel_id=1, source_target_pairs={{0,1},{1,2},{2,3},{3,4},{4,5},{5,6},{6,7},{7,0}} | collective-permute-start | bytes 50331656 | tf_op jit(solution)/shard_map/while/body/eval_jaxpr/ppermute | solution.py:50
  1603.5 93.8 %collective-permute-start = (bf16[4096,1024]{1,0:T(8,128)(2,1)}, bf16[4096,1024]{1,0:T(8,128)(2,1)}, u32[]{:S(2)}, u32[]{:S(2)}) collective-permute-start(bf16[4096,1024]{1,0:T(8,128)(2,1)} %get-tuple-element.205), channel_id=1, source_target_pairs={{0,1},{1,2},{2,3},{3,4},{4,5},{5,6},{6,7},{7,0}} | collective-permute-start | bytes 25165832 | tf_op jit(solution)/shard_map/while/body/eval_jaxpr/ppermute | solution.py:49
  1603.5 273.5 %collective-permute-start.1 = (f32[4096,1024]{1,0:T(8,128)}, f32[4096,1024]{1,0:T(8,128)}, u32[]{:S(2)}, u32[]{:S(2)}) collective-permute-start(f32[4096,1024]{1,0:T(8,128)} %get-tuple-element.206), channel_id=1, source_target_pairs={{0,1},{1,2},{2,3},{3,4},{4,5},{5,6},{6,7},{7,0}} | collective-permute-start | bytes 50331656 | tf_op jit(solution)/shard_map/while/body/eval_jaxpr/ppermute | solution.py:50
  1929.2 93.8 %collective-permute-start = (bf16[4096,1024]{1,0:T(8,128)(2,1)}, bf16[4096,1024]{1,0:T(8,128)(2,1)}, u32[]{:S(2)}, u32[]{:S(2)}) collective-permute-start(bf16[4096,1024]{1,0:T(8,128)(2,1)} %get-tuple-element.205), channel_id=1, source_target_pairs={{0,1},{1,2},{2,3},{3,4},{4,5},{5,6},{6,7},{7,0}} | collective-permute-start | bytes 25165832 | tf_op jit(solution)/shard_map/while/body/eval_jaxpr/ppermute | solution.py:49
  1929.2 273.5 %collective-permute-start.1 = (f32[4096,1024]{1,0:T(8,128)}, f32[4096,1024]{1,0:T(8,128)}, u32[]{:S(2)}, u32[]{:S(2)}) collective-permute-start(f32[4096,1024]{1,0:T(8,128)} %get-tuple-element.206), channel_id=1, source_target_pairs={{0,1},{1,2},{2,3},{3,4},{4,5},{5,6},{6,7},{7,0}} | collective-permute-start | bytes 50331656 | tf_op jit(solution)/shard_map/while/body/eval_jaxpr/ppermute | solution.py:50
  2254.9 93.8 %collective-permute-start = (bf16[4096,1024]{1,0:T(8,128)(2,1)}, bf16[4096,1024]{1,0:T(8,128)(2,1)}, u32[]{:S(2)}, u32[]{:S(2)}) collective-permute-start(bf16[4096,1024]{1,0:T(8,128)(2,1)} %get-tuple-element.205), channel_id=1, source_target_pairs={{0,1},{1,2},{2,3},{3,4},{4,5},{5,6},{6,7},{7,0}} | collective-permute-start | bytes 25165832 | tf_op jit(solution)/shard_map/while/body/eval_jaxpr/ppermute | solution.py:49
  2254.9 273.5 %collective-permute-start.1 = (f32[4096,1024]{1,0:T(8,128)}, f32[4096,1024]{1,0:T(8,128)}, u32[]{:S(2)}, u32[]{:S(2)}) collective-permute-start(f32[4096,1024]{1,0:T(8,128)} %get-tuple-element.206), channel_id=1, source_target_pairs={{0,1},{1,2},{2,3},{3,4},{4,5},{5,6},{6,7},{7,0}} | collective-permute-start | bytes 50331656 | tf_op jit(solution)/shard_map/while/body/eval_jaxpr/ppermute | solution.py:50
  2607.0 183.7 %collective-permute-start.2 = (f32[4096,1024]{0,1:T(8,128)}, f32[4096,1024]{0,1:T(8,128)}, u32[]{:S(2)}, u32[]{:S(2)}) collective-permute-start(f32[4096,1024]{0,1:T(8,128)} %copy.14), channel_id=1, source_target_pairs={{0,1},{1,2},{2,3},{3,4},{4,5},{5,6},{6,7},{7,0}} | collective-permute-start | bytes 50331656 | tf_op jit(solution)/shard_map/ppermute | solution.py:56
  2624.5 188.5 %copy-start.8 = (f32[4096]{0:T(1024)S(1)}, f32[4096]{0:T(1024)}, u32[]{:S(2)}) copy-start(f32[4096]{0:T(1024)} %copy-done.7) | copy-start | bytes 49156
  2624.5 188.5 %copy-start.6 = (f32[4096]{0:T(1024)S(1)}, f32[4096]{0:T(1024)}, u32[]{:S(2)}) copy-start(f32[4096]{0:T(1024)} %copy-done.5) | copy-start | bytes 49156
  2624.5 188.6 %copy-start.12 = (f32[4096]{0:T(1024)S(1)}, f32[4096]{0:T(1024)}, u32[]{:S(2)}) copy-start(f32[4096]{0:T(1024)} %copy-done.11) | copy-start | bytes 49156
  2813.1 22.5 copy-start.10
  2835.6 158.4 %copy-start.1 = (bf16[1280,1024]{1,0:T(8,128)(2,1)S(1)}, bf16[1280,1024]{1,0:T(8,128)(2,1)}, u32[]{:S(2)}) copy-start(bf16[1280,1024]{1,0:T(8,128)(2,1)} %param.10) | copy-start | bytes 7864324
Sparse Core Ops, SparseCore 0:
  2854.6 128.1 all-reduce.3
where the time goes:
time: 3010 us; the launch traced here: 3000 us
  matrix products  1660 us (55%)
  waiting for transfers between devices  1090 us (36%)
  local copies, waits for them, and re-layouts  128 us (4%)
  loops' own time  46.3 us (2%)
  other arithmetic  32.2 us (1%)
    dot_general x8, matrix products, tile_terms(): jnp.einsum('id,jd->ij', img_emb, txt_blk, preferred_element_type=jnp.floa...  815 us
    ppermute x7, waiting for transfers between devices, hop(): txt_blk = lax.ppermute(txt_blk, batch_axes, next_perm)  652 us
    dot_general x8, matrix products, tile_terms(): jnp.einsum('ij,id->jd', grad_b, img_emb, preferred_element_type=jnp.float32)  398 us
    dot_general x8, matrix products, tile_terms(): d_img = jnp.dot(grad_b, txt_blk, preferred_element_type=jnp.float32)  370 us
    ppermute x7, waiting for transfers between devices, hop(): d_txt_acc = lax.ppermute(d_txt_acc, batch_axes, next_perm)  170 us
    ppermute x1, waiting for transfers between devices, local_fn(): d_txt_home = lax.ppermute(final_state[1], batch_axes, next_perm)  166 us
    psum x1, waiting for transfers between devices, local_fn(): lax.psum((final_state[3], final_state[4], final_state[5], d_w_img, d_w_tx...  103 us
  transfers between devices with their start and end apart: 16, of which 16 were waited for; matrix products, arithmetic and copies ran while one was open for 36% of the time, Pallas kernels for 0%

commit v1 on v0

v1 whole, which is shorter than its diff:
```python
import functools
import jax
import jax.numpy as jnp
from jax import lax
from jax.experimental import pallas as pl
from jax.experimental.pallas import tpu as pltpu
from jax.sharding import PartitionSpec as P


LOG2E = 1.4426950408889634
LN2 = 0.6931471805599453
BM, BN = 512, 512
PIECES, SHIFT = 16, 6


def embed_kernel(x_ref, w_ref, emb_ref, raw_ref):
    raw = jnp.dot(x_ref[...], w_ref[...], preferred_element_type=jnp.float32)
    raw_ref[...] = raw
    emb_ref[...] = (raw * lax.rsqrt(jnp.sum(raw * raw, axis=-1, keepdims=True))).astype(jnp.bfloat16)


def embed_call(feat_x, w_proj):
    rows, feat = feat_x.shape
    dim = w_proj.shape[1]
    out_spec = pl.BlockSpec((BN, dim), lambda j: (j, 0))
    return pl.pallas_call(
        embed_kernel,
        grid=(rows // BN,),
        in_specs=[pl.BlockSpec((BN, feat), lambda j: (j, 0)), pl.BlockSpec((feat, dim), lambda j: (0, 0))],
        out_specs=[out_spec, out_spec],
        out_shape=[jax.ShapeDtypeStruct((rows, dim), jnp.bfloat16), jax.ShapeDtypeStruct((rows, dim), jnp.float32)],
        compiler_params=pltpu.CompilerParams(vmem_limit_bytes=40 * 2**20),
        cost_estimate=pl.CostEstimate(flops=2 * rows * feat * dim, bytes_accessed=2 * rows * feat + 6 * rows * dim, transcendentals=0),
        name="embed",
    )(feat_x, w_proj)


def weight_kernel(n_full, sc_ref, x_ref, raw_ref, *refs):
    parts, (first_ref, second_ref, out_ref) = refs[:n_full], refs[n_full:]
    j = pl.program_id(0)
    raw = raw_ref[...]
    inv = lax.rsqrt(jnp.sum(raw * raw, axis=-1, keepdims=True))
    unit = raw * inv
    total = parts[0][...]
    for p in parts[1:]:
        total = total + p[...]
    far = jnp.where(j < pl.num_programs(0) // 2, first_ref[...], second_ref[...])
    d = sc_ref[0] * (total + far)
    d_raw = inv * (d - unit * jnp.sum(unit * d, axis=-1, keepdims=True))
    part = lax.dot_general(x_ref[...], d_raw.astype(jnp.bfloat16), (((0,), (0,)), ((), ())), preferred_element_type=jnp.float32)

    @pl.when(j == 0)
    def _():
        out_ref[...] = part

    @pl.when(j > 0)
    def _():
        out_ref[...] += part


def weight_call(sc, feat_x, raw, parts, first, second):
    rows, feat = feat_x.shape
    dim = raw.shape[1]
    nh = first.shape[0] // BN
    row_spec = pl.BlockSpec((BN, dim), lambda j: (j, 0))
    return pl.pallas_call(
        functools.partial(weight_kernel, len(parts)),
        grid=(rows // BN,),
        in_specs=[pl.BlockSpec(memory_space=pltpu.SMEM), pl.BlockSpec((BN, feat), lambda j: (j, 0)), row_spec]
        + [row_spec] * len(parts)
        + [pl.BlockSpec((BN, dim), lambda j: (jnp.minimum(j, nh - 1), 0)), pl.BlockSpec((BN, dim), lambda j: (jnp.maximum(j - nh, 0), 0))],
        out_specs=pl.BlockSpec((feat, dim), lambda j: (0, 0)),
        out_shape=jax.ShapeDtypeStruct((feat, dim), jnp.float32),
        compiler_params=pltpu.CompilerParams(vmem_limit_bytes=56 * 2**20),
        cost_estimate=pl.CostEstimate(flops=2 * rows * feat * dim, bytes_accessed=2 * rows * feat + 4 * rows * dim * (len(parts) + 2), transcendentals=0),
        name="weight",
    )(sc, feat_x, raw, *parts, first, second)


def tree(x):
    while x.shape[0] > 1:
        x = x.reshape(x.shape[0] // 2, 2, *x.shape[1:])
        x = x[:, 0] + x[:, 1]
    return x[0]


def pair_kernel(m_rows, diag, has_di, has_dt, *refs):
    refs = list(refs)
    sc_ref, i_ref, t_ref = refs[:3]
    refs = refs[3:]
    di_in = refs.pop(0) if has_di else None
    dt_in = refs.pop(0) if has_dt else None
    st_in, di_out, dt_out, st_out, di_acc, g0, g1, in_sem, out_sem = refs
    j = pl.program_id(0)
    last = pl.num_programs(0) - 1
    bm, bn, dim = BM, BN, di_acc.shape[1]
    steps = m_rows // bm
    pr = bm // PIECES
    scale, bias = sc_ref[0], sc_ref[1]

    def rows(k):
        return pl.ds(pl.multiple_of(k * bm, bm), bm)

    def load_di(k):
        return pltpu.make_async_copy(di_in.at[rows(k)], di_acc.at[rows(k)], in_sem.at[k])

    def store_di(k):
        return pltpu.make_async_copy(di_acc.at[rows(k)], di_out.at[rows(k)], out_sem.at[k])

    @pl.when(j == 0)
    def _():
        st_out[...] = st_in[...]
        if has_di:
            @pl.loop(0, steps)
            def _(k):
                load_di(k).start()
        else:
            @pl.loop(0, steps)
            def _(k):
                di_acc[rows(k), :] = jnp.zeros((bm, dim), jnp.float32)

    if has_dt:
        dt_out[...] = dt_in[...]
    else:
        dt_out[...] = jnp.zeros_like(dt_out)

    def dot_s(k):
        return lax.dot_general(i_ref[rows(k), :], t_ref[...], (((1,), (1,)), ((), ())), preferred_element_type=jnp.float32)

    def make_g(k, s_all, g_buf, marks):
        for r in range(PIECES):
            s = s_all[r * pr:(r + 1) * pr, :].reshape(pr // 8, 8, bn)
            if marks is not None and r >= SHIFT:
                b_vec = bias + jnp.concatenate([marks[r - SHIFT] * 0.0] * (bn // 128), axis=1)[None]
            else:
                b_vec = bias
            w = s * scale + b_vec
            if diag:
                rid = lax.broadcasted_iota(jnp.int32, (pr // 8, 8, bn), 0) * 8 + lax.broadcasted_iota(jnp.int32, (pr // 8, 8, bn), 1) + (k * bm + r * pr)
                cid = lax.broadcasted_iota(jnp.int32, (pr // 8, 8, bn), 2) + j * bn
                pos = rid == cid
                w = jnp.where(pos, -w, w)
            a = w * -LOG2E
            g = 1.0 / (1.0 + jnp.exp2(a))
            e = jnp.exp2(-jnp.abs(a))
            u = 1.0 + e
            if diag:
                g = jnp.where(pos, -g, g)
            g_buf[r * pr:(r + 1) * pr, :] = g.reshape(pr, bn).astype(jnp.bfloat16)
            ug = u.reshape(pr // 32, 4, 8, bn)
            st_out[0] += tree(jnp.maximum(w, 0.0) + (e - (u - 1.0)))
            st_out[1] += tree(jnp.log2((ug[:, 0] * ug[:, 1]) * (ug[:, 2] * ug[:, 3])))
            st_out[2] += tree(g * s)
            st_out[3] += tree(g)

    def use_g(k, g_buf):
        g = g_buf[...]
        di = di_acc[rows(k), :] + jnp.dot(g, t_ref[...], preferred_element_type=jnp.float32)
        di_acc[rows(k), :] = di
        dt = dt_out[...] + lax.dot_general(g, i_ref[rows(k), :], (((0,), (0,)), ((), ())), preferred_element_type=jnp.float32)
        dt_out[...] = dt
        marks = []
        for src in (di, dt):
            for p in range(2):
                for h in range(PIECES // 4):
                    r0 = src.shape[0] * 4 // PIECES * h
                    marks.append(src[r0:r0 + 8, p * (dim // 2):p * (dim // 2) + 128])
        return marks

    def both(ks, g_out, ku, g_in):
        s_all = dot_s(ks)
        marks = use_g(ku, g_in)
        make_g(ks, s_all, g_out, marks)

    def before(k):
        if has_di:
            @pl.when(j == 0)
            def _():
                load_di(k).wait()

    def after(k):
        @pl.when(j == last)
        def _():
            store_di(k).start()

    make_g(0, dot_s(0), g0, None)

    @pl.loop(0, steps // 2 - 1)
    def _(p):
        k = 2 * p
        before(k)
        before(k + 1)
        both(k + 1, g1, k, g0)
        both(k + 2, g0, k + 1, g1)
        after(k)
        after(k + 1)

    before(steps - 2)
    before(steps - 1)
    both(steps - 1, g1, steps - 2, g0)
    use_g(steps - 1, g1)
    after(steps - 2)
    after(steps - 1)

    @pl.when(j == last)
    def _():
        @pl.loop(0, steps)
        def _(k):
            store_di(k).wait()


def pair_call(sc, img, txt, di, dt, stats, diag=False):
    m_rows, dim = img.shape
    n_rows = txt.shape[0]
    any_spec = pl.BlockSpec(memory_space=pl.ANY)
    st_spec = pl.BlockSpec((4, 8, BN), lambda j: (0, 0, 0))
    row_spec = pl.BlockSpec((BN, dim), lambda j: (j, 0))
    in_specs = [pl.BlockSpec(memory_space=pltpu.SMEM), pl.BlockSpec((m_rows, dim), lambda j: (0, 0), pipeline_mode=pl.Buffered(1)), row_spec]
    args = [sc, img, txt]
    aliases = {}
    if di is not None:
        aliases[len(args)] = 0
        args.append(di)
        in_specs.append(any_spec)
    if dt is not None:
        aliases[len(args)] = 1
        args.append(dt)
        in_specs.append(row_spec)
    args.append(stats)
    in_specs.append(st_spec)
    pairs = m_rows * n_rows
    return pl.pallas_call(
        functools.partial(pair_kernel, m_rows, diag, di is not None, dt is not None),
        grid=(n_rows // BN,),
        in_specs=in_specs,
        out_specs=[any_spec, row_spec, st_spec],
        out_shape=[jax.ShapeDtypeStruct((m_rows, dim), jnp.float32), jax.ShapeDtypeStruct((n_rows, dim), jnp.float32), jax.ShapeDtypeStruct((4, 8, BN), jnp.float32)],
        scratch_shapes=[pltpu.VMEM((m_rows, dim), jnp.float32), pltpu.VMEM((BM, BN), jnp.bfloat16), pltpu.VMEM((BM, BN), jnp.bfloat16), pltpu.SemaphoreType.DMA((m_rows // BM,)), pltpu.SemaphoreType.DMA((m_rows // BM,))],
        input_output_aliases=aliases,
        compiler_params=pltpu.CompilerParams(vmem_limit_bytes=56 * 2**20),
        cost_estimate=pl.CostEstimate(flops=6 * pairs * dim, bytes_accessed=8 * n_rows * dim + 10 * m_rows * dim, transcendentals=2 * pairs),
        name="pair_diag" if diag else "pair",
    )(*args)


def solution(mesh):
    dev_count = mesh.shape["replica"] * mesh.shape["data"]
    axes = ("replica", "data")

    def swap(x, bit):
        return lax.ppermute(x, axes, [(k, k ^ bit) for k in range(dev_count)])

    core, chip_x, chip_y = 1, 2, 4

    def run(img_x, txt_x, w_img, w_txt, log_temp, logit_bias):
        local_rows = img_x.shape[0]
        total_rows = local_rows * dev_count
        half = local_rows // 2
        temp_scale = jnp.exp(log_temp[0])
        g_scale = temp_scale / total_rows
        sc = jnp.stack([temp_scale, logit_bias[0]])
        t0, txt_raw = embed_call(txt_x, w_txt)
        i0, img_raw = embed_call(img_x, w_img)
        t1 = swap(t0, core)
        t2a, t2b = swap(t0[:half], chip_y), swap(t0[half:], chip_y)
        i1a, i1b = swap(i0[:half], chip_x), swap(i0[half:], chip_x)
        ta = jnp.concatenate([swap(t2a, core), t2a])
        tb = jnp.concatenate([swap(t2b, core), t2b])
        st = jnp.zeros((4, 8, BN), jnp.float32)

        di0, dt0, st = pair_call(sc, i0, t0, None, None, st, diag=True)
        d1a, dt0, st = pair_call(sc, i1a, t0, None, dt0, st)
        d1a, p1, st = pair_call(sc, i1a, t1, d1a, None, st)
        d1a, pa, st = pair_call(sc, i1a, ta, d1a, None, st)
        d1a, pb, st = pair_call(sc, i1a, tb, d1a, None, st)
        xa = swap(d1a, chip_x)
        di0, pa, st = pair_call(sc, i0, ta, di0, pa, st)
        d1b, pa, st = pair_call(sc, i1b, ta, None, pa, st)
        ca = swap(pa[:half], core)
        d1b, dt0, st = pair_call(sc, i1b, t0, d1b, dt0, st)
        ya = swap(pa[half:] + ca, chip_y)
        d1b, pb, st = pair_call(sc, i1b, tb, d1b, pb, st)
        di0, pb, st = pair_call(sc, i0, tb, di0, pb, st)
        cb = swap(pb[:half], core)
        d1b, p1, st = pair_call(sc, i1b, t1, d1b, p1, st)
        xb = swap(d1b, chip_x)
        yb = swap(pb[half:] + cb, chip_y)
        di0, p1, st = pair_call(sc, i0, t1, di0, p1, st)
        back = swap(p1, core)

        sums = lax.psum(jnp.sum(st, axis=(1, 2)), axes)
        gs = jnp.reshape(g_scale, (1,))
        d_w_img = weight_call(gs, img_x, img_raw, (di0,), xa, xb)
        d_w_txt = weight_call(gs, txt_x, txt_raw, (dt0, back), ya, yb)
        d_w_img, d_w_txt = lax.psum((d_w_img, d_w_txt), axes)
        loss_out = jnp.reshape((sums[0] + LN2 * sums[1]) / total_rows, (1,))
        d_log_temp = jnp.reshape(g_scale * sums[2], (1,))
        d_logit_bias = jnp.reshape(sums[3] / total_rows, (1,))
        return loss_out, d_log_temp, d_logit_bias, d_w_img, d_w_txt

    batch_spec = P(axes, None)
    return jax.shard_map(run, mesh=mesh, in_specs=(batch_spec, batch_spec, P(), P(), P(), P()), out_specs=(P(), P(), P(), P(), P()), check_vma=False)
```

time: 3010 us -> 1900 us (0.63)
  matrix products: 1660 us -> 0 us
  Pallas kernels: 0 us -> 1290 us
  waiting for transfers between devices: 1090 us -> 460 us
  local copies, waits for them, and re-layouts: 128 us -> 53.5 us
  loops' own time: 46.3 us -> 0 us
    dot_general x28 -> x0, matrix products: 1660 us -> none  [the longest x8 815 us: tile_terms(): jnp.einsum('id,jd->ij', img_emb, txt_blk, preferred_element_type=jnp.floa...]
    pallas_call x0 -> x16, Pallas kernels: none -> 1290 us  [the longest x12 1200 us: pair_call(): pl.pallas_call(functools.partial(pair_kernel, m_rows, diag, di is not Non...]
    ppermute x15 -> x14, waiting for transfers between devices: 988 us -> 360 us  [swap(): return lax.ppermute(x, axes, [(k, k ^ bit) for k in range(dev_count)])]
    while x11 -> x0, local copies, waits for them, and re-layouts: 112 us -> none  [the longest x4 58.9 us: local_fn(): final_state = lax.fori_loop(1, dev_count, hop, init_state)]
    another operation x1 -> x0, loops' own time: 46.3 us -> none  [local_fn(): final_state = lax.fori_loop(1, dev_count, hop, init_state)]
  transfers between devices with their start and end apart: 16 -> 15, of which waited for: 16 -> 4; matrix products, arithmetic and copies ran while one was open for 36% -> 2% of each run, Pallas kernels for 0% -> 46%
where the time goes in v1:
time: 1900 us; the launch traced here: 1890 us
  Pallas kernels  1290 us (68%)
  waiting for transfers between devices  460 us (24%)
  local copies, waits for them, and re-layouts  53.5 us (3%)
  blocking collectives  24.8 us (1%)
  other arithmetic  24.7 us (1%)
  between operations  22.1 us (1%)
    pallas_call x12, Pallas kernels, pair_call(): pl.pallas_call(functools.partial(pair_kernel, m_rows, diag, di is not Non...  1200 us
    ppermute x14, waiting for transfers between devices, swap(): return lax.ppermute(x, axes, [(k, k ^ bit) for k in range(dev_count)])  360 us
    psum x1, waiting for transfers between devices, run(): d_w_img, d_w_txt = lax.psum((d_w_img, d_w_txt), axes)  100 us
    pallas_call x2, Pallas kernels, weight_call(): pl.pallas_call(functools.partial(weight_kernel, len(parts)), grid=(rows /...  58.9 us
  transfers between devices with their start and end apart: 15, of which 4 were waited for; matrix products, arithmetic and copies ran while one was open for 2% of the time, Pallas kernels for 46%

profile of v1, /device:TPU:0, one launch (start us, length us, event | category | flops | bytes accessed | tf_op | source)
XLA Modules:
  0.0 1887.7 jit_solution(9972351560505406635)
XLA Ops:
  7.2 1.7 copy-done.1
  9.0 16.9 embed.2
  25.8 3.7 fusion
  29.6 2.3 copy-done
  31.9 3.3 collective-permute-start.6
  35.2 16.2 embed.3
  51.5 6.0 fusion.1
  57.5 2.0 collective-permute-start.3
  60.9 0.6 pad_maximum_fusion.refs_0_
  61.5 0.6 broadcast_in_dim.3.refs_3_
  62.1 152.9 %pair_diag.1 = (f32[4096,1024]{1,0:T(8,128)}, f32[4096,1024]{1,0:T(8,128)}, f32[4,8,512]{2,1,0:T(8,128)}) custom-call(f32[2]{0:T(128)} %pad_maximum_fusion.refs_0_, bf16[4096,1024]{1,0:T(8,128)(2,1)} %copy-done, bf16[4096,1024]{1,0:T(8,128)(2,1)} %get-tuple-element.46.refs_2_, f32[4,8,512]{2,1,0:T(8,128)} %broadcast_in_dim.3.refs_3_), custom_call_target="tpu_custom_call" | custom-call | flops 103079215104 | bytes 75497472 | tf_op jit(solution)/shard_map/pair_diag/pallas_call | solution.py:232
  215.2 25.6 %collective-permute-done.1 = bf16[2048,1024]{1,0:T(8,128)(2,1)S(1)} collective-permute-done((bf16[2048,1024]{1,0:T(8,128)(2,1)}, bf16[2048,1024]{1,0:T(8,128)(2,1)S(1)}, u32[]{:S(2)}, u32[]{:S(2)}) %collective-permute-start.1) | collective-permute-done | bytes 4194336 | tf_op jit(solution)/shard_map/ppermute | solution.py:251
  240.9 71.6 %pair.11 = (f32[2048,1024]{1,0:T(8,128)}, f32[4096,1024]{1,0:T(8,128)}, f32[4,8,512]{2,1,0:T(8,128)}) custom-call(f32[2]{0:T(128)} %pad_maximum_fusion.refs_0_, bf16[2048,1024]{1,0:T(8,128)(2,1)} %collective-permute-done.5.refs_1_, bf16[4096,1024]{1,0:T(8,128)(2,1)} %get-tuple-element.46.refs_2_, ...), custom_call_target="tpu_custom_call", output_to_operand_aliasing={{1}: (3, {})} | custom-call | flops 51539607552 | bytes 54525952 | tf_op jit(solution)/shard_map/pair/pallas_call | solution.py:232
  312.5 2.6 constant_dynamic-update-slice_fusion.3
  315.1 2.6 constant_dynamic-update-slice_fusion.2.refs_2_
  317.8 5.7 constant_dynamic-update-slice_fusion.1
  323.4 0.4 constant_dynamic-update-slice_fusion.refs_2_
  323.9 3.2 copy-done.6
  327.1 76.6 %pair.12 = (f32[2048,1024]{1,0:T(8,128)}, f32[4096,1024]{1,0:T(8,128)}, f32[4,8,512]{2,1,0:T(8,128)}) custom-call(f32[2]{0:T(128)} %pad_maximum_fusion.refs_0_, bf16[2048,1024]{1,0:T(8,128)(2,1)} %collective-permute-done.5.refs_1_, bf16[4096,1024]{1,0:T(8,128)(2,1)} %collective-permute-done.refs_2_, ...), custom_call_target="tpu_custom_call", output_to_operand_aliasing={{0}: (3, {})} | custom-call | flops 51539607552 | bytes 54525952 | tf_op jit(solution)/shard_map/pair/pallas_call | solution.py:232
  403.8 76.7 %pair.13 = (f32[2048,1024]{1,0:T(8,128)}, f32[4096,1024]{1,0:T(8,128)}, f32[4,8,512]{2,1,0:T(8,128)}) custom-call(f32[2]{0:T(128)} %pad_maximum_fusion.refs_0_, bf16[2048,1024]{1,0:T(8,128)(2,1)} %collective-permute-done.5.refs_1_, bf16[4096,1024]{1,0:T(8,128)(2,1)} %copy-done.5, ...), custom_call_target="tpu_custom_call", output_to_operand_aliasing={{0}: (3, {})} | custom-call | flops 51539607552 | bytes 54525952 | tf_op jit(solution)/shard_map/pair/pallas_call | solution.py:232
  480.5 76.7 %pair.14 = (f32[2048,1024]{1,0:T(8,128)}, f32[4096,1024]{1,0:T(8,128)}, f32[4,8,512]{2,1,0:T(8,128)}) custom-call(f32[2]{0:T(128)} %pad_maximum_fusion.refs_0_, bf16[2048,1024]{1,0:T(8,128)(2,1)} %collective-permute-done.5.refs_1_, bf16[4096,1024]{1,0:T(8,128)(2,1)} %copy-done.6, ...), custom_call_target="tpu_custom_call", output_to_operand_aliasing={{0}: (3, {})} | custom-call | flops 51539607552 | bytes 54525952 | tf_op jit(solution)/shard_map/pair/pallas_call | solution.py:232
  557.2 146.8 %pair.15 = (f32[4096,1024]{1,0:T(8,128)}, f32[4096,1024]{1,0:T(8,128)}, f32[4,8,512]{2,1,0:T(8,128)}) custom-call(f32[2]{0:T(128)} %pad_maximum_fusion.refs_0_, bf16[4096,1024]{1,0:T(8,128)(2,1)} %copy-done, bf16[4096,1024]{1,0:T(8,128)(2,1)} %copy-done.5, f32[4096,1024]{1,0:T(8,128)} %get-tuple-element.47.refs_3_, ...), custom_call_target="tpu_custom_call", output_to_operand_aliasing={{0}: (3, {}), {1}: (4, {})} | custom-call | flops 103079215104 | bytes 75497472 | tf_op jit(solution)/shard_map/pair/pallas_call | solution.py:232
  704.0 71.3 %pair.16 = (f32[2048,1024]{1,0:T(8,128)}, f32[4096,1024]{1,0:T(8,128)}, f32[4,8,512]{2,1,0:T(8,128)}) custom-call(f32[2]{0:T(128)} %pad_maximum_fusion.refs_0_, bf16[2048,1024]{1,0:T(8,128)(2,1)} %collective-permute-done.6.refs_1_, bf16[4096,1024]{1,0:T(8,128)(2,1)} %copy-done.5, ...), custom_call_target="tpu_custom_call", output_to_operand_aliasing={{1}: (3, {})} | custom-call | flops 51539607552 | bytes 54525952 | tf_op jit(solution)/shard_map/pair/pallas_call | solution.py:232
  775.3 77.7 %pair.17 = (f32[2048,1024]{1,0:T(8,128)}, f32[4096,1024]{1,0:T(8,128)}, f32[4,8,512]{2,1,0:T(8,128)}) custom-call(f32[2]{0:T(128)} %pad_maximum_fusion.refs_0_, bf16[2048,1024]{1,0:T(8,128)(2,1)} %collective-permute-done.6.refs_1_, bf16[4096,1024]{1,0:T(8,128)(2,1)} %get-tuple-element.46.refs_2_, ...), custom_call_target="tpu_custom_call", output_to_operand_aliasing={{0}: (3, {}), {1}: (4, {})} | custom-call | flops 51539607552 | bytes 54525952 | tf_op jit(solution)/shard_map/pair/pallas_call | solution.py:232
  853.0 77.9 %pair.18 = (f32[2048,1024]{1,0:T(8,128)}, f32[4096,1024]{1,0:T(8,128)}, f32[4,8,512]{2,1,0:T(8,128)}) custom-call(f32[2]{0:T(128)} %pad_maximum_fusion.refs_0_, bf16[2048,1024]{1,0:T(8,128)(2,1)} %collective-permute-done.6.refs_1_, bf16[4096,1024]{1,0:T(8,128)(2,1)} %copy-done.6, ...), custom_call_target="tpu_custom_call", output_to_operand_aliasing={{0}: (3, {}), {1}: (4, {})} | custom-call | flops 51539607552 | bytes 54525952 | tf_op jit(solution)/shard_map/pair/pallas_call | solution.py:232
  930.9 146.8 %pair.19 = (f32[4096,1024]{1,0:T(8,128)}, f32[4096,1024]{1,0:T(8,128)}, f32[4,8,512]{2,1,0:T(8,128)}) custom-call(f32[2]{0:T(128)} %pad_maximum_fusion.refs_0_, bf16[4096,1024]{1,0:T(8,128)(2,1)} %copy-done, bf16[4096,1024]{1,0:T(8,128)(2,1)} %copy-done.6, f32[4096,1024]{1,0:T(8,128)} %get-tuple-element.58.refs_3_, ...), custom_call_target="tpu_custom_call", output_to_operand_aliasing={{0}: (3, {}), {1}: (4, {})} | custom-call | flops 103079215104 | bytes 75497472 | tf_op jit(solution)/shard_map/pair/pallas_call | solution.py:232
  1077.8 9.4 slice.47
  1087.2 1.7 copy-done.3
  1089.0 4.1 slice.45
  1093.0 0.5 collective-permute-start.10
  1093.5 77.7 %pair.20 = (f32[2048,1024]{1,0:T(8,128)}, f32[4096,1024]{1,0:T(8,128)}, f32[4,8,512]{2,1,0:T(8,128)}) custom-call(f32[2]{0:T(128)} %pad_maximum_fusion.refs_0_, bf16[2048,1024]{1,0:T(8,128)(2,1)} %collective-permute-done.6.refs_1_, bf16[4096,1024]{1,0:T(8,128)(2,1)} %collective-permute-done.refs_2_, ...), custom_call_target="tpu_custom_call", output_to_operand_aliasing={{0}: (3, {}), {1}: (4, {})} | custom-call | flops 51539607552 | bytes 54525952 | tf_op jit(solution)/shard_map/pair/pallas_call | solution.py:232
  1171.2 146.8 %pair.21 = (f32[4096,1024]{1,0:T(8,128)}, f32[4096,1024]{1,0:T(8,128)}, f32[4,8,512]{2,1,0:T(8,128)}) custom-call(f32[2]{0:T(128)} %pad_maximum_fusion.refs_0_, bf16[4096,1024]{1,0:T(8,128)(2,1)} %copy-done, bf16[4096,1024]{1,0:T(8,128)(2,1)} %collective-permute-done.refs_2_, ...), custom_call_target="tpu_custom_call", output_to_operand_aliasing={{0}: (3, {}), {1}: (4, {})} | custom-call | flops 103079215104 | bytes 75497472 | tf_op jit(solution)/shard_map/pair/pallas_call | solution.py:232
  1318.0 0.5 collective-permute-start.9
  1318.6 1.7 collective-permute-start.7
  1320.3 0.3 collective-permute-start.8
  1320.6 12.0 slice_add_fusion.1
  1332.6 1.7 collective-permute-start.11
  1334.3 12.0 slice_add_fusion
  1346.6 155.6 %collective-permute-done.7.refs_1_ = f32[2048,1024]{1,0:T(8,128)} collective-permute-done((f32[2048,1024]{1,0:T(8,128)}, f32[2048,1024]{1,0:T(8,128)}, u32[]{:S(2)}, u32[]{:S(2)}) %collective-permute-start.7) | collective-permute-done | bytes 8388640 | tf_op jit(solution)/shard_map/ppermute | solution.py:251
  1502.2 178.8 %collective-permute-done.8.refs_2_ = f32[2048,1024]{1,0:T(8,128)} collective-permute-done((f32[2048,1024]{1,0:T(8,128)}, f32[2048,1024]{1,0:T(8,128)}, u32[]{:S(2)}, u32[]{:S(2)}) %collective-permute-start.8) | collective-permute-done | bytes 8388640 | tf_op jit(solution)/shard_map/ppermute | solution.py:251
  1681.0 28.8 %weight.2 = f32[1280,1024]{1,0:T(8,128)} custom-call(f32[1]{0:T(128)S(6)} %div.10.sc_ref, bf16[4096,1280]{1,0:T(8,128)(2,1)} %x_ref.6, f32[4096,1024]{1,0:T(8,128)} %get-tuple-element.76.raw_ref, f32[4096,1024]{1,0:T(8,128)} %get-tuple-element.77.refs_0_, f32[2048,1024]{1,0:T(8,128)} %collective-permute-done.7.refs_1_, ...), custom_call_target="tpu_custom_call" | custom-call | flops 10737418240 | bytes 60817408 | tf_op jit(solution)/shard_map/weight/pallas_call | solution.py:66
  1709.9 30.1 %weight.3 = f32[1024,1024]{1,0:T(8,128)} custom-call(f32[1]{0:T(128)S(6)} %div.10.sc_ref, bf16[4096,1024]{1,0:T(8,128)(2,1)} %x_ref.7, f32[4096,1024]{1,0:T(8,128)} %get-tuple-element.80.raw_ref, f32[4096,1024]{1,0:T(8,128)} %get-tuple-element.81.refs_0_, f32[4096,1024]{1,0:T(8,128)} %collective-permute-done.9.refs_1_, ...), custom_call_target="tpu_custom_call" | custom-call | flops 8589934592 | bytes 75497472 | tf_op jit(solution)/shard_map/weight/pallas_call | solution.py:66
  1740.0 0.8 copy-done.7
  1740.9 24.8 %psum.21 = f32[4]{0:T(128)S(1)} all-reduce(f32[4]{0:T(128)S(1)} %reduce_sum.9), channel_id=1, replica_groups=mesh['replica'=4,'data'=2] {'replica','data'}, use_global_device_ids=true, to_apply=%region_1.0 | all-reduce | flops 4 | bytes 32 | tf_op jit(solution)/shard_map/psum | solution.py:291
  1765.7 0.6 fusion.2
  1768.9 100.3 %all-reduce.3.cloned.1.call-done = (f32[1280,1024]{1,0:T(8,128)}, f32[1024,1024]{1,0:T(8,128)}) async-done(((f32[1280,1024]{1,0:T(8,128)}, f32[1024,1024]{1,0:T(8,128)}), (f32[1280,1024]{1,0:T(8,128)}, f32[1024,1024]{1,0:T(8,128)})) %all-reduce.3.cloned.1.call-update) | async-done | bytes 9437200 | tf_op jit(solution)/shard_map/psum | solution.py:295
  1869.2 5.8 copy.51
  1875.0 2.0 copy.52
  (32 shorter events, 0.8 us)
Async XLA Ops:
  7.2 1862.0 %all-reduce.3.cloned.1.call-start = ((), (), s32[]{:S(2)}) async-start(), calls=%async_computation | async-start | bytes 18874368 | tf_op jit(solution)/shard_map/psum | solution.py:295
  7.2 1.7 copy-start.1
  25.8 6.1 copy-start
  25.8 9.4 copy-start.2
  31.9 672.1 %collective-permute-start.6 = (bf16[2048,1024]{1,0:T(8,128)(2,1)}, bf16[2048,1024]{1,0:T(8,128)(2,1)}, u32[]{:S(2)}, u32[]{:S(2)}) collective-permute-start(bf16[2048,1024]{1,0:T(8,128)(2,1)} %get-tuple-element.87), channel_id=1, source_target_pairs={{0,2},{1,3},{2,0},{3,1},{4,6},{5,7},{6,4},{7,5}} | collective-permute-start | bytes 12582920 | tf_op jit(solution)/shard_map/ppermute | solution.py:251
  35.2 205.7 %collective-permute-start.5 = (bf16[2048,1024]{1,0:T(8,128)(2,1)}, bf16[2048,1024]{1,0:T(8,128)(2,1)}, u32[]{:S(2)}, u32[]{:S(2)}) collective-permute-start(bf16[2048,1024]{1,0:T(8,128)(2,1)} %get-tuple-element.88), channel_id=1, source_target_pairs={{0,2},{1,3},{2,0},{3,1},{4,6},{5,7},{6,4},{7,5}} | collective-permute-start | bytes 12582920 | tf_op jit(solution)/shard_map/ppermute | solution.py:251
  51.5 272.4 %collective-permute-start = (bf16[4096,1024]{1,0:T(8,128)(2,1)}, bf16[4096,1024]{1,0:T(8,128)(2,1)}, u32[]{:S(2)}, u32[]{:S(2)}) collective-permute-start(bf16[4096,1024]{1,0:T(8,128)(2,1)} %get-tuple-element.46.refs_2_), channel_id=1, source_target_pairs={{0,1},{1,0},{2,3},{3,2},{4,5},{5,4},{6,7},{7,6}} | collective-permute-start | bytes 25165832 | tf_op jit(solution)/shard_map/ppermute | solution.py:251
  57.5 157.5 %collective-permute-start.3 = (bf16[2048,1024]{1,0:T(8,128)(2,1)}, bf16[2048,1024]{1,0:T(8,128)(2,1)}, u32[]{:S(2)}, u32[]{:S(2)}) collective-permute-start(bf16[2048,1024]{1,0:T(8,128)(2,1)} %get-tuple-element.89), channel_id=1, source_target_pairs={{0,4},{1,5},{2,6},{3,7},{4,0},{5,1},{6,2},{7,3}} | collective-permute-start | bytes 12582920 | tf_op jit(solution)/shard_map/ppermute | solution.py:251
  59.5 181.3 %collective-permute-start.1 = (bf16[2048,1024]{1,0:T(8,128)(2,1)}, bf16[2048,1024]{1,0:T(8,128)(2,1)S(1)}, u32[]{:S(2)}, u32[]{:S(2)}) collective-permute-start(bf16[2048,1024]{1,0:T(8,128)(2,1)} %get-tuple-element.90), channel_id=1, source_target_pairs={{0,4},{1,5},{2,6},{3,7},{4,0},{5,1},{6,2},{7,3}} | collective-permute-start | bytes 12582920 | tf_op jit(solution)/shard_map/ppermute | solution.py:251
  215.0 97.5 %collective-permute-start.4 = (bf16[2048,1024]{1,0:T(8,128)(2,1)}, bf16[2048,1024]{1,0:T(8,128)(2,1)}, u32[]{:S(2)}, u32[]{:S(2)}) collective-permute-start(bf16[2048,1024]{1,0:T(8,128)(2,1)} %collective-permute-done.3), channel_id=1, source_target_pairs={{0,1},{1,0},{2,3},{3,2},{4,5},{5,4},{6,7},{7,6}} | collective-permute-start | bytes 12582920 | tf_op jit(solution)/shard_map/ppermute | solution.py:251
  240.9 76.9 %collective-permute-start.2 = (bf16[2048,1024]{1,0:T(8,128)(2,1)S(1)}, bf16[2048,1024]{1,0:T(8,128)(2,1)}, u32[]{:S(2)}, u32[]{:S(2)}) collective-permute-start(bf16[2048,1024]{1,0:T(8,128)(2,1)S(1)} %collective-permute-done.1), channel_id=1, source_target_pairs={{0,1},{1,0},{2,3},{3,2},{4,5},{5,4},{6,7},{7,6}} | collective-permute-start | bytes 12582920 | tf_op jit(solution)/shard_map/ppermute | solution.py:251
  317.7 6.1 copy-start.5
  323.9 3.2 copy-start.6
  1077.8 11.2 copy-start.3
  1093.0 227.6 %collective-permute-start.10 = (f32[2048,1024]{1,0:T(8,128)}, f32[2048,1024]{1,0:T(8,128)}, u32[]{:S(2)}, u32[]{:S(2)}) collective-permute-start(f32[2048,1024]{1,0:T(8,128)} %slice.45), channel_id=1, source_target_pairs={{0,1},{1,0},{2,3},{3,2},{4,5},{5,4},{6,7},{7,6}} | collective-permute-start | bytes 25165832 | tf_op jit(solution)/shard_map/ppermute | solution.py:251
  1093.5 240.8 %collective-permute-start.12 = (f32[2048,1024]{1,0:T(8,128)}, f32[2048,1024]{1,0:T(8,128)}, u32[]{:S(2)}, u32[]{:S(2)}) collective-permute-start(f32[2048,1024]{1,0:T(8,128)} %slice.47), channel_id=1, source_target_pairs={{0,1},{1,0},{2,3},{3,2},{4,5},{5,4},{6,7},{7,6}} | collective-permute-start | bytes 25165832 | tf_op jit(solution)/shard_map/ppermute | solution.py:251
  1318.0 391.8 %collective-permute-start.9 = (f32[4096,1024]{1,0:T(8,128)}, f32[4096,1024]{1,0:T(8,128)}, u32[]{:S(2)}, u32[]{:S(2)}) collective-permute-start(f32[4096,1024]{1,0:T(8,128)} %get-tuple-element.82), channel_id=1, source_target_pairs={{0,1},{1,0},{2,3},{3,2},{4,5},{5,4},{6,7},{7,6}} | collective-permute-start | bytes 50331656 | tf_op jit(solution)/shard_map/ppermute | solution.py:251
  1318.6 183.6 %collective-permute-start.7 = (f32[2048,1024]{1,0:T(8,128)}, f32[2048,1024]{1,0:T(8,128)}, u32[]{:S(2)}, u32[]{:S(2)}) collective-permute-start(f32[2048,1024]{1,0:T(8,128)} %get-tuple-element.78), channel_id=1, source_target_pairs={{0,2},{1,3},{2,0},{3,1},{4,6},{5,7},{6,4},{7,5}} | collective-permute-start | bytes 25165832 | tf_op jit(solution)/shard_map/ppermute | solution.py:251
  1320.3 360.8 %collective-permute-start.8 = (f32[2048,1024]{1,0:T(8,128)}, f32[2048,1024]{1,0:T(8,128)}, u32[]{:S(2)}, u32[]{:S(2)}) collective-permute-start(f32[2048,1024]{1,0:T(8,128)} %get-tuple-element.79), channel_id=1, source_target_pairs={{0,2},{1,3},{2,0},{3,1},{4,6},{5,7},{6,4},{7,5}} | collective-permute-start | bytes 25165832 | tf_op jit(solution)/shard_map/ppermute | solution.py:251
  1332.6 377.3 %collective-permute-start.11 = (f32[2048,1024]{1,0:T(8,128)}, f32[2048,1024]{1,0:T(8,128)}, u32[]{:S(2)}, u32[]{:S(2)}) collective-permute-start(f32[2048,1024]{1,0:T(8,128)} %slice_add_fusion.1), channel_id=1, source_target_pairs={{0,4},{1,5},{2,6},{3,7},{4,0},{5,1},{6,2},{7,3}} | collective-permute-start | bytes 25165832 | tf_op jit(solution)/shard_map/ppermute | solution.py:251
  1346.3 363.5 %collective-permute-start.13 = (f32[2048,1024]{1,0:T(8,128)}, f32[2048,1024]{1,0:T(8,128)}, u32[]{:S(2)}, u32[]{:S(2)}) collective-permute-start(f32[2048,1024]{1,0:T(8,128)} %slice_add_fusion), channel_id=1, source_target_pairs={{0,4},{1,5},{2,6},{3,7},{4,0},{5,1},{6,2},{7,3}} | collective-permute-start | bytes 25165832 | tf_op jit(solution)/shard_map/ppermute | solution.py:251
  1740.0 0.8 copy-start.7
  1869.2 5.9 copy-start.4
Sparse Core Ops, SparseCore 0:
  1740.1 129.0 all-reduce.2
